TPU v7x, 1024 devices: a whole 4x8x16 slice. The times are simulated.
1024 devices in a mesh: curve: 128 (over y, z), group: 8 (over x, core).
Axes of the slice: x: 4, y: 8, z: 16, core: 2. Of those that a mesh axis runs over, the one named last changes fastest.
Arguments:
- position: float32 [3, 16384, 128], P(None, ('curve', 'group')), may hold values from 0 to 2048
- mass: float32 [16384, 128], P(('curve', 'group')), may hold values from 0.003 to 0.03
- smooth: float32 [16384, 128], P(('curve', 'group')), may hold values from 0.25 to 1
- counts: int32 [16384], P(('curve', 'group')), may hold values from 8 to 128
- partners: int32 [16384, 8], P('curve'), may hold values from 0 to 16383, as said below
Outputs:
- density: float32 [16384, 128], P(('curve', 'group'))
- accel: float32 [3, 16384, 128], P(None, ('curve', 'group'))
Inputs may be any that keep to these rules, and one draw needn't show every extreme that they name: partners[a, k] is a cell other than a whose distance to a along the cyclic curve order is 1 to 7; the 8 entries of a row differ.
All inputs are finite; a program needn't handle non-finite values.
Results may differ from a plain program's by a relative error of at most 0.0003.
Values sent between devices are 32-bit elements; how exact they have to be, the bound alone decides.
No kernel may reach another device: no remote copies, remote signals or barrier semaphores. Data moves between devices by JAX's collectives and lax.ppermute only.
A program may use at most 32 MiB of HBM per device.

v0:
```python
import math

import jax
import jax.numpy as jnp
from jax import lax
from jax.sharding import PartitionSpec as P

REACH = 7


def padded(x, sides, width):
    for axis, dim in sides:
        devices, length = (lax.axis_size(axis), x.shape[dim])
        up = [(i, (i + 1) % devices) for i in range(devices)]
        down = [(j, i) for i, j in up]
        last = lax.slice_in_dim(x, length - width, length, axis=dim)
        leading = lax.slice_in_dim(x, 0, width, axis=dim)
        before = lax.ppermute(last, axis, up)
        after = lax.ppermute(leading, axis, down)
        x = jnp.concatenate([before, x, after], axis=dim)
    return x


def pair_sums(tpos, tsmooth, trecip, lists, table, force):
    count = lists.shape[0]
    width = lists.shape[1]
    slots = tpos.shape[-1]
    rows = table.shape[0]
    block = math.gcd(count, 4)
    blocks = count // block
    tp = tpos.reshape(3, blocks, block, slots).transpose(1, 0, 2, 3)
    tsb = tsmooth.reshape(blocks, block, slots)
    trb = trecip.reshape(blocks, block, slots)
    lsb = lists.reshape(blocks, block * width)

    def one(items):
        here, smooth_h, recip_h, listed = items
        source = jnp.take(table, listed, axis=1).reshape(rows, block, width * slots)
        delta = here[:, :, :, None] - source[:3, :, None, :]
        inv_sq = 1.0 / (smooth_h * smooth_h)
        weight = jnp.exp(-jnp.sum(delta * delta, 0) * inv_sq[..., None])
        if force:
            coeff = source[3][:, None, :] * (recip_h[..., None] + source[4][:, None, :]) * weight
            return 2.0 * inv_sq * jnp.sum(coeff * delta, -1)
        return jnp.sum(source[3][:, None, :] * weight, -1) * inv_sq / smooth_h

    result = lax.map(one, (tp, tsb, trb, lsb))
    if force:
        return result.transpose(1, 0, 2, 3).reshape(3, count, slots)
    return result.reshape(count, slots)


def shards(position, mass, smooth, counts, partners):
    groups = lax.axis_size("group")
    gidx = lax.axis_index("group")
    cidx = lax.axis_index("curve")
    own_cells = counts.shape[0]
    span = own_cells * groups
    total = span * lax.axis_size("curve")
    slots = position.shape[-1]
    alive = jnp.arange(slots, dtype=jnp.int32)[None, :] < counts[:, None]
    zero_own = jnp.zeros_like(mass)
    mlive = jnp.where(alive, mass, zero_own)
    own_rows = gidx * own_cells
    start = cidx * span + own_rows
    packed = jnp.concatenate([position, mlive[None]], 0)
    rim = padded(packed, ((("curve", "group"), 1),), REACH)
    mine = lax.dynamic_slice_in_dim(partners, own_rows, own_cells, 0)
    local = (mine - start + REACH) % total
    own_lists = (REACH + jnp.arange(own_cells, dtype=jnp.int32))[:, None]
    lists = jnp.concatenate([own_lists, local], 1)
    density = pair_sums(position, smooth, zero_own, lists, rim, False)
    density = jnp.where(alive, density, zero_own)
    recip_own = jnp.where(alive, 1.0 / jnp.where(alive, density, jnp.ones_like(density)), zero_own)
    recip_rim = padded(recip_own, ((("curve", "group"), 0),), REACH)
    table_f = jnp.concatenate([rim, recip_rim[None]], 0)
    accel = pair_sums(position, smooth, recip_own, lists, table_f, True)
    accel = jnp.where(alive[None], accel, jnp.zeros_like(accel))
    return (density, accel)


def solution(mesh):
    return jax.shard_map(
        shards,
        mesh=mesh,
        in_specs=(
            P(None, ("curve", "group"), None),
            P(("curve", "group"), None),
            P(("curve", "group"), None),
            P(("curve", "group")),
            P("curve", None),
        ),
        out_specs=(P(("curve", "group"), None), P(None, ("curve", "group"), None)),
        check_vma=False,
    )
```

profile of v0, /device:TPU:32, one launch (start us, length us, event | category | flops | bytes accessed | tf_op | source)
XLA Modules:
  0.0 71.9 jit_solution(10442676286018749941)
XLA Ops:
  0.6 0.8 %copy.28 = f32[3,16,128]{2,0,1:T(4,128)S(1)} copy(f32[3,16,128]{2,1,0:T(8,128)} %param.9) | data formatting | bytes 49152 | tf_op args[0]
  1.4 0.8 %fusion.10 = f32[16,128]{1,0:T(8,128)S(1)} fusion(f32[16,128]{1,0:T(8,128)} %param.10, s32[16]{0:T(128)} %param.12), kind=kLoop, calls=%fused_computation.52 | loop fusion | flops 4096 | bytes 16448 | tf_op jit(solution)/shard_map/jit(_where)/select_n | solution.py:63
  2.2 1.9 %collective-permute-start = (f32[4,7,128]{2,0,1:T(4,128)S(1)}, f32[4,7,128]{2,0,1:T(4,128)S(1)}, u32[]{:S(2)}, u32[]{:S(2)}) collective-permute-start(f32[4,7,128]{2,0,1:T(4,128)S(1)} %get-tuple-element.145), channel_id=1, source_target_pairs={{0,1},{1,2},{2,3},{3,4},{4,5},{5,6},{6,7},{7,8},{8,9},{9,10},{10,1... | collective-permute-start | bytes 43016 | tf_op jit(solution)/shard_map/ppermute | solution.py:18
  4.1 19.7 %collective-permute-start.1 = (f32[4,7,128]{2,0,1:T(4,128)S(1)}, f32[4,7,128]{2,0,1:T(4,128)S(1)}, u32[]{:S(2)}, u32[]{:S(2)}) collective-permute-start(f32[4,7,128]{2,0,1:T(4,128)S(1)} %get-tuple-element.146), channel_id=1, source_target_pairs={{1,0},{2,1},{3,2},{4,3},{5,4},{6,5},{7,6},{8,7},{9,8},{10,9},{11,1... | collective-permute-start | bytes 43016 | tf_op jit(solution)/shard_map/ppermute | solution.py:19
  23.9 0.7 %iota_compare_fusion.1 = pred[16,128]{1,0:T(8,128)(4,1)S(1)} fusion(s32[16]{0:T(128)} %param.12), kind=kLoop, calls=%fused_computation.50 | loop fusion | flops 2048 | bytes 2112 | tf_op jit(solution)/shard_map/lt | solution.py:61
  24.6 0.8 %add_select_fusion = s32[16,8]{0,1:T(8,128)S(1)} fusion(s32[128,8]{0,1:T(8,128)} %param.13, s32[]{:T(128)S(6)} %select_n.75, s32[]{:T(128)S(6)} %add.99), kind=kLoop, calls=%fused_computation.53 | loop fusion | flops 1664 | bytes 1032 | tf_op jit(solution)/shard_map/jit(remainder)/select_n | solution.py:69
  25.4 0.7 %lt.89 = s32[4,4]{1,0:T(4,128)S(1)} reshape(s32[16]{0:T(128)} %param.12) | data formatting | bytes 128 | tf_op jit(solution)/shard_map/lt | solution.py:61
  26.3 0.7 %copy.30 = f32[4,3,4,128]{3,2,1,0:T(4,128)S(1)} copy(f32[4,3,4,128]{3,2,0,1:T(4,128)} %bitcast.101) | data formatting | bytes 49152 | tf_op jit(solution)/shard_map/while | solution.py:47
  27.1 14.8 %while.22 = (s32[]{:T(128)}, f32[4,4,128]{2,1,0:T(4,128)S(1)}, s32[4,36]{1,0:T(4,128)S(1)}, f32[4,30,128]{2,0,1:T(4,128)S(1)}, f32[4,3,4,128]{3,2,1,0:T(4,128)S(1)}, /*index=5*/f32[4,4,128]{2,1,0:T(4,128)}) while((s32[]{:T(128)}, f32[4,4,128]{2,1,0:T(4,128)S(1)}, s32[4,36]{1,0:T(4,128)S(1)}, f32[4,30,128]{2,0,1:T(4,128)S(1)}, ...), condition=%wide.region_3.4_spmd.clone, body=%wide.region_0.3_spmd.sunk.clone | while | flops 7100230 | bytes 5419897 | solution.py:47
  27.1 0.7 fusion.29
  28.7 0.7 %multiply_reduce_fusion.6 = f32[4,128,1152]{2,1,0:T(8,128)S(1)} fusion(f32[3,4,1152]{2,1,0:T(4,128)S(1)} %sub.84, f32[3,4,128]{2,1,0:T(4,128)S(1)} %dynamic-slice_bitcast_fusion.7), kind=kLoop, calls=%fused_computation.2.clone.1.clone | loop fusion | flops 4718592 | bytes 2420736 | tf_op jit(solution)/shard_map/while/body/eval_jaxpr/reduce_sum | solution.py:41
  29.4 0.7 multiply_reduce_fusion.7
  30.1 0.7 fusion.30
  30.8 0.7 fusion.29
  32.4 0.7 %multiply_reduce_fusion.6 = f32[4,128,1152]{2,1,0:T(8,128)S(1)} fusion(f32[3,4,1152]{2,1,0:T(4,128)S(1)} %sub.84, f32[3,4,128]{2,1,0:T(4,128)S(1)} %dynamic-slice_bitcast_fusion.7), kind=kLoop, calls=%fused_computation.2.clone.1.clone | loop fusion | flops 4718592 | bytes 2420736 | tf_op jit(solution)/shard_map/while/body/eval_jaxpr/reduce_sum | solution.py:41
  33.1 0.7 multiply_reduce_fusion.7
  33.8 0.7 fusion.30
  34.5 0.7 fusion.29
  35.2 0.6 gather_fusion
  36.1 0.7 %multiply_reduce_fusion.6 = f32[4,128,1152]{2,1,0:T(8,128)S(1)} fusion(f32[3,4,1152]{2,1,0:T(4,128)S(1)} %sub.84, f32[3,4,128]{2,1,0:T(4,128)S(1)} %dynamic-slice_bitcast_fusion.7), kind=kLoop, calls=%fused_computation.2.clone.1.clone | loop fusion | flops 4718592 | bytes 2420736 | tf_op jit(solution)/shard_map/while/body/eval_jaxpr/reduce_sum | solution.py:41
  36.8 0.7 multiply_reduce_fusion.7
  37.5 0.7 fusion.30
  38.2 0.7 fusion.29
  39.8 0.7 %multiply_reduce_fusion.6 = f32[4,128,1152]{2,1,0:T(8,128)S(1)} fusion(f32[3,4,1152]{2,1,0:T(4,128)S(1)} %sub.84, f32[3,4,128]{2,1,0:T(4,128)S(1)} %dynamic-slice_bitcast_fusion.7), kind=kLoop, calls=%fused_computation.2.clone.1.clone | loop fusion | flops 4718592 | bytes 2420736 | tf_op jit(solution)/shard_map/while/body/eval_jaxpr/reduce_sum | solution.py:41
  40.5 0.7 multiply_reduce_fusion.7
  41.2 0.7 fusion.30
  41.9 0.7 divide_select_fusion.1
  42.6 1.9 %collective-permute-start.2 = (f32[7,128]{1,0:T(8,128)S(1)}, f32[7,128]{1,0:T(8,128)S(1)}, u32[]{:S(2)}, u32[]{:S(2)}) collective-permute-start(f32[7,128]{1,0:T(8,128)S(1)} %get-tuple-element.147), channel_id=1, source_target_pairs={{0,1},{1,2},{2,3},{3,4},{4,5},{5,6},{6,7},{7,8},{8,9},{9,10},{10,1... | collective-permute-start | bytes 10760 | tf_op jit(solution)/shard_map/ppermute | solution.py:18
  44.5 9.1 %collective-permute-start.3 = (f32[7,128]{1,0:T(8,128)S(1)}, f32[7,128]{1,0:T(8,128)S(1)}, u32[]{:S(2)}, u32[]{:S(2)}) collective-permute-start(f32[7,128]{1,0:T(8,128)S(1)} %get-tuple-element.148), channel_id=1, source_target_pairs={{1,0},{2,1},{3,2},{4,3},{5,4},{6,5},{7,6},{8,7},{9,8},{10,9},{11,1... | collective-permute-start | bytes 10760 | tf_op jit(solution)/shard_map/ppermute | solution.py:19
  53.7 1.2 %collective-permute-done.3 = f32[7,128]{1,0:T(8,128)S(1)} collective-permute-done((f32[7,128]{1,0:T(8,128)S(1)}, f32[7,128]{1,0:T(8,128)S(1)}, u32[]{:S(2)}, u32[]{:S(2)}) %collective-permute-start.3) | collective-permute-done | bytes 3616 | tf_op jit(solution)/shard_map/ppermute | solution.py:19
  55.0 16.3 %while.23 = (s32[]{:T(128)}, f32[4,3,4,128]{3,2,1,0:T(4,128)S(1)}, f32[4,4,128]{2,1,0:T(4,128)}, s32[4,36]{1,0:T(4,128)S(1)}, f32[5,30,128]{2,0,1:T(8,128)S(1)},...) while((s32[]{:T(128)}, f32[4,3,4,128]{3,2,1,0:T(4,128)S(1)}, f32[4,4,128]{2,1,0:T(4,128)}, ...), condition=%wide.region_7.8_spmd.clone, body=%wide.region_4.7_spmd.sunk.clone | while | flops 13002054 | bytes 10496897 | solution.py:47
  55.0 0.7 multiply_bitcast_fusion.3
  56.7 0.8 %fusion.32 = f32[4,128,1152]{2,1,0:T(8,128)S(1)} fusion(f32[3,4,1152]{2,1,0:T(4,128)S(1)} %sub.91, f32[3,4,128]{2,1,0:T(4,128)S(1)} %dynamic-slice_bitcast_fusion.8), kind=kLoop, calls=%fused_computation.20.clone.1.clone | loop fusion | flops 4718592 | bytes 2420736 | tf_op jit(solution)/shard_map/while/body/eval_jaxpr/reduce_sum | solution.py:41
  57.4 0.7 exponential_multiply_fusion.3
  58.1 0.9 %fusion.33 = f32[3,4,128]{2,1,0:T(4,128)S(1)} fusion(f32[4,128,1152]{2,1,0:T(8,128)S(1)} %exponential_multiply_fusion.3, f32[3,4,1152]{2,1,0:T(4,128)S(1)} %sub.91, f32[3,4,128]{2,1,0:T(4,128)S(1)} %dynamic-slice_bitcast_fusion.8), kind=kLoop, calls=%fused_computation.21.clone.1.clone | loop fusion | flops 5306880 | bytes 2426880 | tf_op jit(solution)/shard_map/while/body/eval_jaxpr/reduce_sum | solution.py:44
  59.1 0.7 multiply_bitcast_fusion.3
  60.7 0.8 %fusion.32 = f32[4,128,1152]{2,1,0:T(8,128)S(1)} fusion(f32[3,4,1152]{2,1,0:T(4,128)S(1)} %sub.91, f32[3,4,128]{2,1,0:T(4,128)S(1)} %dynamic-slice_bitcast_fusion.8), kind=kLoop, calls=%fused_computation.20.clone.1.clone | loop fusion | flops 4718592 | bytes 2420736 | tf_op jit(solution)/shard_map/while/body/eval_jaxpr/reduce_sum | solution.py:41
  61.5 0.7 exponential_multiply_fusion.3
  62.2 0.9 %fusion.33 = f32[3,4,128]{2,1,0:T(4,128)S(1)} fusion(f32[4,128,1152]{2,1,0:T(8,128)S(1)} %exponential_multiply_fusion.3, f32[3,4,1152]{2,1,0:T(4,128)S(1)} %sub.91, f32[3,4,128]{2,1,0:T(4,128)S(1)} %dynamic-slice_bitcast_fusion.8), kind=kLoop, calls=%fused_computation.21.clone.1.clone | loop fusion | flops 5306880 | bytes 2426880 | tf_op jit(solution)/shard_map/while/body/eval_jaxpr/reduce_sum | solution.py:44
  63.2 0.7 multiply_bitcast_fusion.3
  64.8 0.8 %fusion.32 = f32[4,128,1152]{2,1,0:T(8,128)S(1)} fusion(f32[3,4,1152]{2,1,0:T(4,128)S(1)} %sub.91, f32[3,4,128]{2,1,0:T(4,128)S(1)} %dynamic-slice_bitcast_fusion.8), kind=kLoop, calls=%fused_computation.20.clone.1.clone | loop fusion | flops 4718592 | bytes 2420736 | tf_op jit(solution)/shard_map/while/body/eval_jaxpr/reduce_sum | solution.py:41
  65.6 0.7 exponential_multiply_fusion.3
  66.3 0.9 %fusion.33 = f32[3,4,128]{2,1,0:T(4,128)S(1)} fusion(f32[4,128,1152]{2,1,0:T(8,128)S(1)} %exponential_multiply_fusion.3, f32[3,4,1152]{2,1,0:T(4,128)S(1)} %sub.91, f32[3,4,128]{2,1,0:T(4,128)S(1)} %dynamic-slice_bitcast_fusion.8), kind=kLoop, calls=%fused_computation.21.clone.1.clone | loop fusion | flops 5306880 | bytes 2426880 | tf_op jit(solution)/shard_map/while/body/eval_jaxpr/reduce_sum | solution.py:44
  67.2 0.7 multiply_bitcast_fusion.3
  68.9 0.8 %fusion.32 = f32[4,128,1152]{2,1,0:T(8,128)S(1)} fusion(f32[3,4,1152]{2,1,0:T(4,128)S(1)} %sub.91, f32[3,4,128]{2,1,0:T(4,128)S(1)} %dynamic-slice_bitcast_fusion.8), kind=kLoop, calls=%fused_computation.20.clone.1.clone | loop fusion | flops 4718592 | bytes 2420736 | tf_op jit(solution)/shard_map/while/body/eval_jaxpr/reduce_sum | solution.py:41
  69.6 0.7 exponential_multiply_fusion.3
  70.3 0.9 %fusion.33 = f32[3,4,128]{2,1,0:T(4,128)S(1)} fusion(f32[4,128,1152]{2,1,0:T(8,128)S(1)} %exponential_multiply_fusion.3, f32[3,4,1152]{2,1,0:T(4,128)S(1)} %sub.91, f32[3,4,128]{2,1,0:T(4,128)S(1)} %dynamic-slice_bitcast_fusion.8), kind=kLoop, calls=%fused_computation.21.clone.1.clone | loop fusion | flops 5306880 | bytes 2426880 | tf_op jit(solution)/shard_map/while/body/eval_jaxpr/reduce_sum | solution.py:44
  71.3 0.6 broadcast_select_fusion
  (110 shorter events, 6.9 us)
Async XLA Ops:
  2.2 24.9 %collective-permute-start = (f32[4,7,128]{2,0,1:T(4,128)S(1)}, f32[4,7,128]{2,0,1:T(4,128)S(1)}, u32[]{:S(2)}, u32[]{:S(2)}) collective-permute-start(f32[4,7,128]{2,0,1:T(4,128)S(1)} %get-tuple-element.145), channel_id=1, source_target_pairs={{0,1},{1,2},{2,3},{3,4},{4,5},{5,6},{6,7},{7,8},{8,9},{9,10},{10,1... | collective-permute-start | bytes 43016 | tf_op jit(solution)/shard_map/ppermute | solution.py:18
  4.1 22.9 %collective-permute-start.1 = (f32[4,7,128]{2,0,1:T(4,128)S(1)}, f32[4,7,128]{2,0,1:T(4,128)S(1)}, u32[]{:S(2)}, u32[]{:S(2)}) collective-permute-start(f32[4,7,128]{2,0,1:T(4,128)S(1)} %get-tuple-element.146), channel_id=1, source_target_pairs={{1,0},{2,1},{3,2},{4,3},{5,4},{6,5},{7,6},{8,7},{9,8},{10,9},{11,1... | collective-permute-start | bytes 43016 | tf_op jit(solution)/shard_map/ppermute | solution.py:19
  27.1 14.8 %copy-start = (s32[16]{0:T(128)S(1)}, s32[16]{0:T(128)}, u32[]{:S(2)}) copy-start(s32[16]{0:T(128)} %param.12) | copy-start | bytes 196
  42.6 11.1 %collective-permute-start.2 = (f32[7,128]{1,0:T(8,128)S(1)}, f32[7,128]{1,0:T(8,128)S(1)}, u32[]{:S(2)}, u32[]{:S(2)}) collective-permute-start(f32[7,128]{1,0:T(8,128)S(1)} %get-tuple-element.147), channel_id=1, source_target_pairs={{0,1},{1,2},{2,3},{3,4},{4,5},{5,6},{6,7},{7,8},{8,9},{9,10},{10,1... | collective-permute-start | bytes 10760 | tf_op jit(solution)/shard_map/ppermute | solution.py:18
  44.5 10.4 %collective-permute-start.3 = (f32[7,128]{1,0:T(8,128)S(1)}, f32[7,128]{1,0:T(8,128)S(1)}, u32[]{:S(2)}, u32[]{:S(2)}) collective-permute-start(f32[7,128]{1,0:T(8,128)S(1)} %get-tuple-element.148), channel_id=1, source_target_pairs={{1,0},{2,1},{3,2},{4,3},{5,4},{6,5},{7,6},{8,7},{9,8},{10,9},{11,1... | collective-permute-start | bytes 10760 | tf_op jit(solution)/shard_map/ppermute | solution.py:19
where the time goes:
time: 72.6 us; the launch traced here: 71.9 us
  starting transfers between devices  32.6 us (45%)
  other arithmetic  28.1 us (39%)
  local copies, waits for them, and re-layouts  8.39 us (12%)
  waiting for transfers between devices  1.23 us (2%)
  between operations  0.74 us (1%)
  loops' own time  0.73 us (1%)
    ppermute x2, starting transfers between devices, padded(): after = lax.ppermute(leading, axis, down)  28.8 us
    reduce_sum x8, other arithmetic, one(): weight = jnp.exp(-jnp.sum(delta * delta, 0) * inv_sq[..., None])  6 us
    gather x8, local copies, waits for them, and re-layouts, one(): source = jnp.take(table, listed, axis=1).reshape(rows, block, width * slots)  4.82 us
    ppermute x2, starting transfers between devices, padded(): before = lax.ppermute(last, axis, up)  3.83 us
    reduce_sum x4, other arithmetic, one(): return 2.0 * inv_sq * jnp.sum(coeff * delta, -1)  3.5 us
    dynamic_update_slice x8, other arithmetic, pair_sums(): result = lax.map(one, (tp, tsb, trb, lsb))  2.85 us
    mul x4, other arithmetic, one(): source[3][:, None, :] * (recip_h[..., None] + source[4][:, None, :])  2.83 us
    mul x4, other arithmetic, one(): return 2.0 * inv_sq * jnp.sum(coeff * delta, -1)  2.77 us
  transfers between devices with their start and end apart: 4, of which 1 were waited for; matrix products, arithmetic and copies ran while one was open for 4% of the time, Pallas kernels for 0%

commit v1 on v0

v1 whole, which is shorter than its diff:
```python
import functools

import jax, jax.numpy as jnp
from jax import lax
from jax.experimental import pallas as pl
from jax.experimental.pallas import tpu as pltpu
from jax.sharding import PartitionSpec as P

LOG2E = 1.4426950408889634
HI = lax.Precision.HIGHEST
TABLE = 48
OWN = 16
CURVE = 128
NCELL = 16384
REACH = 7
KP = 8
X, Y, Z, M, H, S, R = range(7)


def body(odd_of, own, mate, peer, dens_ref, acc_ref, tab, bc, wts, part, row_f, ids, sems):
    odd = odd_of()
    sides = ((1, own), (2 - 2 * odd, mate), (2 * odd, peer))
    copies = []
    for n, (side, src) in enumerate(sides):
        copy = pltpu.make_async_copy(src.at[pl.ds(80, 8), :], ids.at[side], sems.at[n])
        copy.start()
        copies.append(copy)
    for side, src in sides:
        h = src[64:80, :]
        s = -LOG2E / (h * h)
        for p in range(16):
            for c in range(5):
                tab[side * 16 + p, c, :] = src[c * 16 + p, :]
            tab[side * 16 + p, S, :] = s[p]

    def columns(e, slot, chans):
        t = tab[e].T
        for n, c in chans:
            bc[slot, n] = jnp.broadcast_to(t[:, c : c + 1], (128, 128))

    def spread(i, _):
        columns(9 + i, i, ((0, X), (1, Y), (2, Z), (3, S)))
        return 0

    lax.fori_loop(0, 30, spread, 0, unroll=2)
    for copy in copies:
        copy.wait()

    def partner(e, k):
        side = e // 16
        return e + ids[side, k, e % 16].astype(jnp.int32)

    def bcast(e, c):
        return tab[e, pl.ds(c, 8, stride=0), :][None]

    def dens_cell(i, store):
        e = 9 + i
        who = [e] + [partner(e, k) for k in range(KP)]
        for g in range(4):
            rows = pl.ds(32 * g, 32)
            xi, yi, zi, si = [bc[i, n, rows, :].reshape(4, 8, 128) for n in range(4)]
            total = jnp.zeros((4, 8, 128), jnp.float32)
            for k, j in enumerate(who):
                dx = xi - bcast(j, X)
                dy = yi - bcast(j, Y)
                dz = zi - bcast(j, Z)
                w = jnp.exp2((dx * dx + dy * dy + dz * dz) * si) * bcast(j, M)
                total = total + w
                if store:
                    wts[i - 7, k, rows, :] = w.reshape(32, 128)
            part[i, rows, :] = total.reshape(32, 128)

    def own_dens(i, _):
        dens_cell(7 + i, True)
        return 0

    def rim_dens(i, _):
        dens_cell(jnp.where(i < 7, i, i + 16), False)
        return 0

    lax.fori_loop(0, 16, own_dens, 0)
    lax.fori_loop(0, 14, rim_dens, 0)
    ones = jnp.ones((8, 128), jnp.float32)

    def rowsum(v):
        return lax.dot_general(ones, v, (((1,), (1,)), ((), ())), precision=HI, preferred_element_type=jnp.float32)

    def finish(i, _):
        e = 9 + i
        t = rowsum(part[i])[0:1]
        h = tab[e, pl.ds(H, 1), :]
        live = tab[e, pl.ds(M, 1), :] > 0.0
        d = jnp.where(live, t / (h * h * h), 0.0)
        row_f[i] = jnp.broadcast_to(d, (8, 128))
        tab[e, pl.ds(R, 1), :] = jnp.where(live, 1.0 / jnp.where(live, d, 1.0), 0.0)
        return 0

    lax.fori_loop(0, 30, finish, 0, unroll=3)
    for p in range(16):
        dens_ref[p, :] = row_f[7 + p, 0]

    def spread_r(i, _):
        columns(16 + i, 7 + i, ((3, R),))
        return 0

    lax.fori_loop(0, 16, spread_r, 0, unroll=2)

    def force_cell(i, _):
        e = 16 + i
        who = [e] + [partner(e, k) for k in range(KP)]
        for g in range(4):
            rows = pl.ds(32 * g, 32)
            xi, yi, zi, ri = [bc[7 + i, n, rows, :].reshape(4, 8, 128) for n in range(4)]
            fx = fy = fz = jnp.zeros((4, 8, 128), jnp.float32)
            for k, j in enumerate(who):
                c = wts[i, k, rows, :].reshape(4, 8, 128) * (ri + bcast(j, R))
                fx = fx + c * (xi - bcast(j, X))
                fy = fy + c * (yi - bcast(j, Y))
                fz = fz + c * (zi - bcast(j, Z))
            bc[7 + i, 0, rows, :] = fx.reshape(32, 128)
            bc[7 + i, 1, rows, :] = fy.reshape(32, 128)
            bc[7 + i, 2, rows, :] = fz.reshape(32, 128)
        return 0

    lax.fori_loop(0, 16, force_cell, 0)

    def finish_f(i, _):
        e = 16 + i
        s = tab[e, pl.ds(S, 1), :]
        live = tab[e, pl.ds(M, 1), :] > 0.0
        scale = jnp.where(live, s * (-2.0 / LOG2E), 0.0)
        for n in range(3):
            row_f[i, n] = (rowsum(bc[7 + i, n])[0:1] * scale)[0]
        return 0

    lax.fori_loop(0, 16, finish_f, 0, unroll=2)
    for p in range(16):
        for n in range(3):
            acc_ref[n, p, :] = row_f[p, n]


def call(own, mate, peer, odd_of):
    f32 = jnp.float32
    return pl.pallas_call(
        functools.partial(body, odd_of),
        out_shape=(jax.ShapeDtypeStruct((16, 128), f32), jax.ShapeDtypeStruct((3, 16, 128), f32)),
        in_specs=[pl.BlockSpec(memory_space=pltpu.VMEM)] * 3,
        out_specs=(pl.BlockSpec(memory_space=pltpu.VMEM),) * 2,
        scratch_shapes=[
            pltpu.VMEM((TABLE, 8, 128), f32),
            pltpu.VMEM((30, 4, 128, 128), f32),
            pltpu.VMEM((16, 9, 128, 128), f32),
            pltpu.VMEM((30, 128, 128), f32),
            pltpu.VMEM((30, 8, 128), f32),
            pltpu.SMEM((3, 8, 128), f32),
            pltpu.SemaphoreType.DMA((3,)),
        ],
        compiler_params=pltpu.CompilerParams(vmem_limit_bytes=48 << 20),
        name="sph",
    )(own, mate, peer)


def shards(position, mass, smooth, counts, partners):
    groups = lax.axis_size("group")
    devices = groups * lax.axis_size("curve")
    group = lax.axis_index("group")
    start = lax.axis_index("curve") * CURVE
    slots = position.shape[-1]
    alive = jnp.arange(slots, dtype=jnp.int32)[None, :] < counts[:, None]
    mlive = jnp.where(alive, mass, jnp.zeros_like(mass))
    step = partners.T - (start + jnp.arange(CURVE, dtype=jnp.int32))[None, :]
    step = jnp.where(step > REACH, step - NCELL, jnp.where(step < -REACH, step + NCELL, step))
    step = lax.dynamic_slice_in_dim(step.astype(jnp.float32), group * OWN, OWN, 1)
    step = jnp.pad(step, ((0, 0), (0, slots - OWN)))
    packed = jnp.concatenate([position.reshape(3 * OWN, slots), mlive, smooth, step], 0)
    axes = ("curve", "group")
    chip = [(i, i ^ 1) for i in range(devices)]
    link = [(i, (i + 1 if i % 2 else i - 1) % devices) for i in range(devices)]
    over_link = lax.ppermute(packed, axes, link)
    over_chip = lax.ppermute(packed, axes, chip)
    return call(packed, over_chip, over_link, lambda: lax.rem(lax.axis_index("group"), 2))


def solution(mesh):
    return jax.shard_map(
        shards,
        mesh=mesh,
        in_specs=(
            P(None, ("curve", "group"), None),
            P(("curve", "group"), None),
            P(("curve", "group"), None),
            P(("curve", "group")),
            P("curve", None),
        ),
        out_specs=(P(("curve", "group"), None), P(None, ("curve", "group"), None)),
        check_vma=False,
    )
```

time: 72.6 us -> 57.1 us (0.79)
  the two profiles are of different devices: /device:TPU:32 before, /device:TPU:1 now
where the time goes in v1:
time: 57.1 us; the launch traced here: 56.8 us
  Pallas kernels  27.7 us (49%)
  starting transfers between devices  26.2 us (46%)
  local copies, waits for them, and re-layouts  1.35 us (2%)
  waiting for transfers between devices  0.85 us (1%)
  between operations  0.71 us (1%)
    pallas_call x1, Pallas kernels, call(): pl.pallas_call(functools.partial(body, odd_of), out_shape=(jax.ShapeDtype...  27.7 us
    ppermute x1, starting transfers between devices, shards(): over_chip = lax.ppermute(packed, axes, chip)  21.7 us
    ppermute x1, starting transfers between devices, shards(): over_link = lax.ppermute(packed, axes, link)  4.49 us
    unnamed x10, local copies, waits for them, and re-layouts  1.27 us
  transfers between devices with their start and end apart: 2, of which 1 were waited for; matrix products, arithmetic and copies ran while one was open for 0% of the time, Pallas kernels for 0%

profile of v1, /device:TPU:1, one launch (start us, length us, event | category | flops | bytes accessed | tf_op | source)
XLA Modules:
  0.0 56.8 jit_solution(7323644914229152612)
XLA Ops:
  0.6 0.0 copy-start.3
  0.6 0.0 copy-start.1
  0.7 0.0 copy-start.4
  0.7 0.0 copy-start
  0.7 0.6 %copy-done.3 = s32[128,8]{0,1:T(8,128)S(1)} copy-done((s32[128,8]{0,1:T(8,128)S(1)}, s32[128,8]{0,1:T(8,128)}, u32[]{:S(2)}) %copy-start.3) | copy-done | bytes 4120
  1.3 0.1 constant_dynamic-slice_fusion
  1.4 0.0 copy-done.1
  1.4 0.0 copy-done.4
  1.4 0.0 copy-start.2
  1.4 0.1 fusion
  1.5 0.0 copy-done
  1.5 0.6 %copy-done.2 = f32[16,128]{1,0:T(8,128)S(1)} copy-done((f32[16,128]{1,0:T(8,128)S(1)}, f32[16,128]{1,0:T(8,128)}, u32[]{:S(2)}) %copy-start.2) | copy-done | bytes 8216
  2.1 4.5 %collective-permute-start.1 = (f32[88,128]{1,0:T(8,128)S(1)}, f32[88,128]{1,0:T(8,128)S(1)}, u32[]{:S(2)}, u32[]{:S(2)}) collective-permute-start(f32[88,128]{1,0:T(8,128)S(1)} %select_maximum_fusion.own), channel_id=1, source_target_pairs={{0,1023},{1,2},{2,1},{3,4},{4,3},{5,6},{6,5},{7,8},{8,7},{9,10},{1... | collective-permute-start | bytes 135176 | tf_op jit(solution)/shard_map/ppermute | solution.py:179
  6.6 21.7 %collective-permute-start = (f32[88,128]{1,0:T(8,128)S(1)}, f32[88,128]{1,0:T(8,128)S(1)}, u32[]{:S(2)}, u32[]{:S(2)}) collective-permute-start(f32[88,128]{1,0:T(8,128)S(1)} %select_maximum_fusion.own), channel_id=1, source_target_pairs={{0,1},{1,0},{2,3},{3,2},{4,5},{5,4},{6,7},{7,6},{8,9},{9,8},{10,11... | collective-permute-start | bytes 135176 | tf_op jit(solution)/shard_map/ppermute | solution.py:180
  28.3 0.0 collective-permute-done.1.peer
  28.3 0.8 %collective-permute-done.mate = f32[88,128]{1,0:T(8,128)S(1)} collective-permute-done((f32[88,128]{1,0:T(8,128)S(1)}, f32[88,128]{1,0:T(8,128)S(1)}, u32[]{:S(2)}, u32[]{:S(2)}) %collective-permute-start) | collective-permute-done | bytes 45088 | tf_op jit(solution)/shard_map/ppermute | solution.py:180
  29.1 27.7 %sph.1 = (f32[16,128]{1,0:T(8,128)}, f32[3,16,128]{2,1,0:T(8,128)}) custom-call(f32[88,128]{1,0:T(8,128)S(1)} %select_maximum_fusion.own, f32[88,128]{1,0:T(8,128)S(1)} %collective-permute-done.mate, f32[88,128]{1,0:T(8,128)S(1)} %collective-permute-done.1.peer), custom_call_target="tpu_custom_call" | custom-call | tf_op jit(solution)/shard_map/sph/pallas_call | solution.py:144
  (3 shorter events, 0.0 us)
Async XLA Ops:
  0.6 0.7 %copy-start.3 = (s32[128,8]{0,1:T(8,128)S(1)}, s32[128,8]{0,1:T(8,128)}, u32[]{:S(2)}) copy-start(s32[128,8]{0,1:T(8,128)} %param.9) | copy-start | bytes 12292
  0.6 0.8 %copy-start.1 = (f32[16,128]{1,0:T(8,128)S(1)}, f32[16,128]{1,0:T(8,128)}, u32[]{:S(2)}) copy-start(f32[16,128]{1,0:T(8,128)} %param.6) | copy-start | bytes 24580
  0.7 0.8 %copy-start.4 = (s32[16]{0:T(128)S(1)}, s32[16]{0:T(128)}, u32[]{:S(2)}) copy-start(s32[16]{0:T(128)} %param.8) | copy-start | bytes 196
  0.7 0.8 %copy-start = (f32[3,16,128]{2,1,0:T(8,128)S(1)}, f32[3,16,128]{2,1,0:T(8,128)}, u32[]{:S(2)}) copy-start(f32[3,16,128]{2,1,0:T(8,128)} %param.5) | copy-start | bytes 73732
  1.4 0.7 %copy-start.2 = (f32[16,128]{1,0:T(8,128)S(1)}, f32[16,128]{1,0:T(8,128)}, u32[]{:S(2)}) copy-start(f32[16,128]{1,0:T(8,128)} %param.7) | copy-start | bytes 24580
  2.1 26.2 %collective-permute-start.1 = (f32[88,128]{1,0:T(8,128)S(1)}, f32[88,128]{1,0:T(8,128)S(1)}, u32[]{:S(2)}, u32[]{:S(2)}) collective-permute-start(f32[88,128]{1,0:T(8,128)S(1)} %select_maximum_fusion.own), channel_id=1, source_target_pairs={{0,1023},{1,2},{2,1},{3,4},{4,3},{5,6},{6,5},{7,8},{8,7},{9,10},{1... | collective-permute-start | bytes 135176 | tf_op jit(solution)/shard_map/ppermute | solution.py:179
  6.6 22.5 %collective-permute-start = (f32[88,128]{1,0:T(8,128)S(1)}, f32[88,128]{1,0:T(8,128)S(1)}, u32[]{:S(2)}, u32[]{:S(2)}) collective-permute-start(f32[88,128]{1,0:T(8,128)S(1)} %select_maximum_fusion.own), channel_id=1, source_target_pairs={{0,1},{1,0},{2,3},{3,2},{4,5},{5,4},{6,7},{7,6},{8,9},{9,8},{10,11... | collective-permute-start | bytes 135176 | tf_op jit(solution)/shard_map/ppermute | solution.py:180

commit v2 on v1

--- a/solution.py
+++ b/solution.py
@@ -15,16 +15,14 @@
 REACH = 7
 KP = 8
 X, Y, Z, M, H, S, R = range(7)
-
-
-def body(odd_of, own, mate, peer, dens_ref, acc_ref, tab, bc, wts, part, row_f, ids, sems):
-    odd = odd_of()
-    sides = ((1, own), (2 - 2 * odd, mate), (2 * odd, peer))
-    copies = []
-    for n, (side, src) in enumerate(sides):
-        copy = pltpu.make_async_copy(src.at[pl.ds(80, 8), :], ids.at[side], sems.at[n])
-        copy.start()
-        copies.append(copy)
+CM, CH, CS = 3, 4, 5
+
+
+def partner(ids, e, k):
+    return e + ids[e // 16, k, e % 16].astype(jnp.int32)
+
+
+def direct(sides, dens_ref, acc_ref, tab, bc, wts, part, row_f, ids):
     for side, src in sides:
         h = src[64:80, :]
         s = -LOG2E / (h * h)
@@ -43,19 +41,12 @@
         return 0
 
     lax.fori_loop(0, 30, spread, 0, unroll=2)
-    for copy in copies:
-        copy.wait()
-
-    def partner(e, k):
-        side = e // 16
-        return e + ids[side, k, e % 16].astype(jnp.int32)
-
     def bcast(e, c):
         return tab[e, pl.ds(c, 8, stride=0), :][None]
 
     def dens_cell(i, store):
         e = 9 + i
-        who = [e] + [partner(e, k) for k in range(KP)]
+        who = [e] + [partner(ids, e, k) for k in range(KP)]
         for g in range(4):
             rows = pl.ds(32 * g, 32)
             xi, yi, zi, si = [bc[i, n, rows, :].reshape(4, 8, 128) for n in range(4)]
@@ -107,7 +98,7 @@
 
     def force_cell(i, _):
         e = 16 + i
-        who = [e] + [partner(e, k) for k in range(KP)]
+        who = [e] + [partner(ids, e, k) for k in range(KP)]
         for g in range(4):
             rows = pl.ds(32 * g, 32)
             xi, yi, zi, ri = [bc[7 + i, n, rows, :].reshape(4, 8, 128) for n in range(4)]
@@ -139,6 +130,147 @@
             acc_ref[n, p, :] = row_f[p, n]
 
 
+def split3(t):
+    hi = t.astype(jnp.bfloat16).astype(jnp.float32)
+    rest = t - hi
+    mid = rest.astype(jnp.bfloat16).astype(jnp.float32)
+    return hi, mid, (rest - mid).astype(jnp.bfloat16).astype(jnp.float32)
+
+
+def expanded(dens_ref, acc_ref, com, tj, ti, left, right, rhs, whi, wlo, dsum, val, out, ids):
+    bf16, f32 = jnp.bfloat16, jnp.float32
+    lane = lax.broadcasted_iota(jnp.int32, (128, 128), 1)
+
+    def columns(i, _):
+        hi, mid, lo = split3(tj[2 + i])
+        zero = jnp.zeros((8, 128), f32)
+        half = [hi, mid, hi, lo, hi, mid, zero, zero]
+        t = jnp.concatenate(half + half, 0).T
+        left[2 + i] = jnp.where(lane < 64, t, 0.0).astype(bf16)
+        right[2 + i] = jnp.where(lane < 64, 0.0, t).astype(bf16)
+        return 0
+
+    lax.fori_loop(0, 44, columns, 0, unroll=4)
+
+    def rows(e):
+        hi, mid, lo = split3(ti[e])
+        zero = jnp.zeros((8, 128), f32)
+        return jnp.concatenate([hi, hi, mid, hi, lo, mid, zero, zero], 0).astype(bf16)
+
+    rim = [(0, 1), (2, 3), (4, 5), (6, 23), (24, 25), (26, 27), (28, 29)]
+    blank = jnp.zeros((64, 128), bf16)
+    for t, (i, j) in enumerate([(7 + 2 * t, 8 + 2 * t) for t in range(8)] + rim):
+        rhs[t, 0:64, 0:128] = rows(9 + i)
+        rhs[t, 0:64, 128:256] = blank
+        rhs[t, 64:128, 0:128] = blank
+        rhs[t, 64:128, 128:256] = rows(9 + j)
+
+    def weights(t, i, j, store):
+        a, b = 9 + i, 9 + j
+        r = rhs[t]
+        total = jnp.zeros((8, 256), f32)
+        for k in range(KP + 1):
+            p = a if k == 0 else partner(ids, a, k - 1)
+            q = b if k == 0 else partner(ids, b, k - 1)
+            e = jnp.dot(left[p] + right[q], r, preferred_element_type=f32)
+            w = jnp.exp2(e)
+            total = total + w.reshape(16, 8, 256).sum(0)
+            if store:
+                hi = w.astype(bf16)
+                lo = (w - hi.astype(f32)).astype(bf16)
+                at = pl.ds(128 * k, 128)
+                whi[i - 7, at, :] = hi[:, :128]
+                whi[j - 7, at, :] = hi[:, 128:]
+                wlo[i - 7, at, :] = lo[:, :128]
+                wlo[j - 7, at, :] = lo[:, 128:]
+        dsum[i] = total[:, :128]
+        dsum[j] = total[:, 128:]
+
+    def own_pair(t, _):
+        weights(t, 7 + 2 * t, 8 + 2 * t, True)
+        return 0
+
+    def rim_pair(t, _):
+        i = jnp.where(t > 3, 16 + 2 * t, 2 * t)
+        j = jnp.where(t > 2, 17 + 2 * t, 2 * t + 1)
+        weights(8 + t, i, j, False)
+        return 0
+
+    lax.fori_loop(0, 8, own_pair, 0)
+    lax.fori_loop(0, 7, rim_pair, 0)
+
+    total = sum(dsum[:, n, :] for n in range(8))
+    h = com[CH, 9:39, :]
+    live = com[CM, 9:39, :] > 0.0
+    dens = jnp.where(live, total / (h * h * h), 0.0)
+    recip = jnp.where(live, 1.0 / jnp.where(live, dens, 1.0), 0.0)
+    dens_ref[...] = dens[7:23]
+    sub = lax.broadcasted_iota(jnp.int32, (8, 128), 0)
+    zero = jnp.zeros((8, 128), f32)
+    for i in range(30):
+        t = tj[9 + i]
+        v = jnp.where(sub < 4, t, pltpu.roll(t, 4, 0) * recip[i : i + 1])
+        val[9 + i] = jnp.concatenate([*split3(v), zero], 0).astype(bf16)
+
+    def force(i, _):
+        e = 16 + i
+        who = [e] + [partner(ids, e, k) for k in range(KP)]
+        v = jnp.concatenate([val[j] for j in who], 1)
+        o = jnp.dot(v, whi[i], preferred_element_type=f32) + jnp.dot(v, wlo[i], preferred_element_type=f32)
+        out[i] = o[0:8] + o[8:16] + o[16:24]
+        return 0
+
+    lax.fori_loop(0, 16, force, 0, unroll=2)
+    s = com[CS, 16:32, :]
+    scale = jnp.where(live[7:23], s * (-2.0 / LOG2E), 0.0)
+    r = recip[7:23]
+    for n in range(3):
+        u = com[n, 16:32, :]
+        acc_ref[n] = scale * (r * (u * out[:, 0, :] - out[:, 1 + n, :]) + (u * out[:, 4, :] - out[:, 5 + n, :]))
+
+
+def body(odd_of, own, mate, peer, dens_ref, acc_ref, com, tj, ti, left, right, rhs, whi, wlo, dsum, val, out,
+         tab, bc, wts, part, row_f, ids, sems):
+    odd = odd_of()
+    sides = ((1, own), (2 - 2 * odd, mate), (2 * odd, peer))
+    copies = []
+    for n, (side, src) in enumerate(sides):
+        copy = pltpu.make_async_copy(src.at[pl.ds(80, 8), :], ids.at[side], sems.at[n])
+        copy.start()
+        copies.append(copy)
+    one = jnp.ones((1, 128), jnp.float32)
+    centre = [jnp.broadcast_to(own[16 * c + 8 : 16 * c + 9, 0:1], (16, 128)) for c in range(3)]
+    far = steep = jnp.zeros((16, 128), jnp.float32)
+    for side, src in sides:
+        u = [src[16 * c : 16 * c + 16, :] - centre[c] for c in range(3)]
+        m = src[48:64, :]
+        h = src[64:80, :]
+        s = -LOG2E / (h * h)
+        q = u[0] * u[0] + u[1] * u[1] + u[2] * u[2]
+        lm = jnp.where(m > 0.0, jnp.log2(jnp.where(m > 0.0, m, 1.0)), -30000.0)
+        far = jnp.maximum(far, q)
+        steep = jnp.maximum(steep, -s)
+        at = pl.ds(pl.multiple_of(side * 16, 16), 16)
+        for c, x in enumerate((*u, m, h, s)):
+            com[c, at, :] = x
+        fi = (s * q, -2.0 * s * u[0], -2.0 * s * u[1], -2.0 * s * u[2], s)
+        for p in range(16):
+            e = side * 16 + p
+            tj[e] = jnp.concatenate([one, *(x[p : p + 1] for x in (*u, q, lm)), 0.0 * one, 0.0 * one], 0)
+            ti[e] = jnp.concatenate([*(x[p : p + 1] for x in fi), one, 0.0 * one, 0.0 * one], 0)
+    near = jnp.max(far) * jnp.max(steep) < 2048.0
+    for copy in copies:
+        copy.wait()
+
+    @pl.when(near)
+    def _():
+        expanded(dens_ref, acc_ref, com, tj, ti, left, right, rhs, whi, wlo, dsum, val, out, ids)
+
+    @pl.when(jnp.logical_not(near))
+    def _():
+        direct(sides, dens_ref, acc_ref, tab, bc, wts, part, row_f, ids)
+
+
 def call(own, mate, peer, odd_of):
     f32 = jnp.float32
     return pl.pallas_call(
@@ -147,6 +279,17 @@
         in_specs=[pl.BlockSpec(memory_space=pltpu.VMEM)] * 3,
         out_specs=(pl.BlockSpec(memory_space=pltpu.VMEM),) * 2,
         scratch_shapes=[
+            pltpu.VMEM((6, TABLE, 128), f32),
+            pltpu.VMEM((TABLE, 8, 128), f32),
+            pltpu.VMEM((TABLE, 8, 128), f32),
+            pltpu.VMEM((TABLE, 128, 128), jnp.bfloat16),
+            pltpu.VMEM((TABLE, 128, 128), jnp.bfloat16),
+            pltpu.VMEM((15, 128, 256), jnp.bfloat16),
+            pltpu.VMEM((16, 1152, 128), jnp.bfloat16),
+            pltpu.VMEM((16, 1152, 128), jnp.bfloat16),
+            pltpu.VMEM((30, 8, 128), f32),
+            pltpu.VMEM((TABLE, 32, 128), jnp.bfloat16),
+            pltpu.VMEM((16, 8, 128), f32),
             pltpu.VMEM((TABLE, 8, 128), f32),
             pltpu.VMEM((30, 4, 128, 128), f32),
             pltpu.VMEM((16, 9, 128, 128), f32),
@@ -155,7 +298,7 @@
             pltpu.SMEM((3, 8, 128), f32),
             pltpu.SemaphoreType.DMA((3,)),
         ],
-        compiler_params=pltpu.CompilerParams(vmem_limit_bytes=48 << 20),
+        compiler_params=pltpu.CompilerParams(vmem_limit_bytes=56 << 20),
         name="sph",
     )(own, mate, peer)
 

time: 57.1 us -> 41.8 us (0.73)
  Pallas kernels: 27.7 us -> 11.7 us
  local copies, waits for them, and re-layouts: 1.35 us -> 1.97 us
    pallas_call x1, Pallas kernels: 27.7 us -> 11.7 us  [call(): pl.pallas_call(functools.partial(body, odd_of), out_shape=(jax.ShapeDtype...]
    unnamed x10 -> x16, local copies, waits for them, and re-layouts: 1.27 us -> 1.9 us
where the time goes in v2:
time: 41.8 us; the launch traced here: 41.5 us
  starting transfers between devices  26.2 us (63%)
  Pallas kernels  11.7 us (28%)
  local copies, waits for them, and re-layouts  1.97 us (5%)
  waiting for transfers between devices  0.84 us (2%)
  between operations  0.72 us (2%)
    ppermute x1, starting transfers between devices, shards(): over_chip = lax.ppermute(packed, axes, chip)  21.7 us
    pallas_call x1, Pallas kernels, call(): pl.pallas_call(functools.partial(body, odd_of), out_shape=(jax.ShapeDtype...  11.7 us
    ppermute x1, starting transfers between devices, shards(): over_link = lax.ppermute(packed, axes, link)  4.49 us
    unnamed x16, local copies, waits for them, and re-layouts  1.9 us
  transfers between devices with their start and end apart: 2, of which 1 were waited for; matrix products, arithmetic and copies ran while one was open for 0% of the time, Pallas kernels for 0%

profile of v2, /device:TPU:1, one launch (start us, length us, event | category | flops | bytes accessed | tf_op | source)
XLA Modules:
  0.0 41.5 jit_solution(15053627438781494254)
XLA Ops:
  0.6 0.0 copy-start.6
  0.6 0.0 copy-start.4
  0.7 0.0 copy-start.7
  0.7 0.0 copy-start.3
  0.7 0.6 %copy-done.6 = s32[128,8]{0,1:T(8,128)S(1)} copy-done((s32[128,8]{0,1:T(8,128)S(1)}, s32[128,8]{0,1:T(8,128)}, u32[]{:S(2)}) %copy-start.6) | copy-done | bytes 4120
  1.3 0.1 constant_dynamic-slice_fusion
  1.4 0.0 copy-done.4
  1.4 0.0 copy-done.7
  1.4 0.0 copy-start.5
  1.4 0.1 fusion
  1.5 0.0 copy-done.3
  1.5 0.6 %copy-done.5 = f32[16,128]{1,0:T(8,128)S(1)} copy-done((f32[16,128]{1,0:T(8,128)S(1)}, f32[16,128]{1,0:T(8,128)}, u32[]{:S(2)}) %copy-start.5) | copy-done | bytes 8216
  2.1 0.0 copy-start
  2.1 4.5 %collective-permute-start.1 = (f32[88,128]{1,0:T(8,128)S(1)}, f32[88,128]{1,0:T(8,128)S(1)}, u32[]{:S(2)}, u32[]{:S(2)}) collective-permute-start(f32[88,128]{1,0:T(8,128)S(1)} %select_maximum_fusion.own), channel_id=1, source_target_pairs={{0,1023},{1,2},{2,1},{3,4},{4,3},{5,6},{6,5},{7,8},{8,7},{9,10},{1... | collective-permute-start | bytes 135176 | tf_op jit(solution)/shard_map/ppermute | solution.py:322
  6.6 21.7 %collective-permute-start = (f32[88,128]{1,0:T(8,128)S(1)}, f32[88,128]{1,0:T(8,128)S(1)}, u32[]{:S(2)}, u32[]{:S(2)}) collective-permute-start(f32[88,128]{1,0:T(8,128)S(1)} %select_maximum_fusion.own), channel_id=1, source_target_pairs={{0,1},{1,0},{2,3},{3,2},{4,5},{5,4},{6,7},{7,6},{8,9},{9,8},{10,11... | collective-permute-start | bytes 135176 | tf_op jit(solution)/shard_map/ppermute | solution.py:323
  28.3 0.0 collective-permute-done.1.peer
  28.3 0.0 copy-start.1
  28.3 0.8 %collective-permute-done.mate = f32[88,128]{1,0:T(8,128)S(1)} collective-permute-done((f32[88,128]{1,0:T(8,128)S(1)}, f32[88,128]{1,0:T(8,128)S(1)}, u32[]{:S(2)}, u32[]{:S(2)}) %collective-permute-start) | collective-permute-done | bytes 45088 | tf_op jit(solution)/shard_map/ppermute | solution.py:323
  29.1 0.0 copy-done
  29.1 0.0 copy-done.1
  29.1 0.0 copy-start.2
  29.1 0.6 %copy-done.2 = f32[88,128]{1,0:T(8,128)} copy-done((f32[88,128]{1,0:T(8,128)}, f32[88,128]{1,0:T(8,128)S(1)}, u32[]{:S(2)}) %copy-start.2) | copy-done | bytes 45080
  29.8 11.7 %sph.1 = (f32[16,128]{1,0:T(8,128)}, f32[3,16,128]{2,1,0:T(8,128)}) custom-call(f32[88,128]{1,0:T(8,128)} %copy-done, f32[88,128]{1,0:T(8,128)} %copy-done.2, f32[88,128]{1,0:T(8,128)} %copy-done.1), custom_call_target="tpu_custom_call" | custom-call | tf_op jit(solution)/shard_map/sph/pallas_call | solution.py:276
  (3 shorter events, 0.0 us)
Async XLA Ops:
  0.6 0.7 %copy-start.6 = (s32[128,8]{0,1:T(8,128)S(1)}, s32[128,8]{0,1:T(8,128)}, u32[]{:S(2)}) copy-start(s32[128,8]{0,1:T(8,128)} %param.9) | copy-start | bytes 12292
  0.6 0.8 %copy-start.4 = (f32[16,128]{1,0:T(8,128)S(1)}, f32[16,128]{1,0:T(8,128)}, u32[]{:S(2)}) copy-start(f32[16,128]{1,0:T(8,128)} %param.6) | copy-start | bytes 24580
  0.7 0.8 %copy-start.7 = (s32[16]{0:T(128)S(1)}, s32[16]{0:T(128)}, u32[]{:S(2)}) copy-start(s32[16]{0:T(128)} %param.8) | copy-start | bytes 196
  0.7 0.8 %copy-start.3 = (f32[3,16,128]{2,1,0:T(8,128)S(1)}, f32[3,16,128]{2,1,0:T(8,128)}, u32[]{:S(2)}) copy-start(f32[3,16,128]{2,1,0:T(8,128)} %param.5) | copy-start | bytes 73732
  1.4 0.7 %copy-start.5 = (f32[16,128]{1,0:T(8,128)S(1)}, f32[16,128]{1,0:T(8,128)}, u32[]{:S(2)}) copy-start(f32[16,128]{1,0:T(8,128)} %param.7) | copy-start | bytes 24580
  2.1 27.0 %copy-start = (f32[88,128]{1,0:T(8,128)}, f32[88,128]{1,0:T(8,128)S(1)}, u32[]{:S(2)}) copy-start(f32[88,128]{1,0:T(8,128)S(1)} %select_maximum_fusion.own) | copy-start | bytes 135172
  2.1 26.2 %collective-permute-start.1 = (f32[88,128]{1,0:T(8,128)S(1)}, f32[88,128]{1,0:T(8,128)S(1)}, u32[]{:S(2)}, u32[]{:S(2)}) collective-permute-start(f32[88,128]{1,0:T(8,128)S(1)} %select_maximum_fusion.own), channel_id=1, source_target_pairs={{0,1023},{1,2},{2,1},{3,4},{4,3},{5,6},{6,5},{7,8},{8,7},{9,10},{1... | collective-permute-start | bytes 135176 | tf_op jit(solution)/shard_map/ppermute | solution.py:322
  6.6 22.5 %collective-permute-start = (f32[88,128]{1,0:T(8,128)S(1)}, f32[88,128]{1,0:T(8,128)S(1)}, u32[]{:S(2)}, u32[]{:S(2)}) collective-permute-start(f32[88,128]{1,0:T(8,128)S(1)} %select_maximum_fusion.own), channel_id=1, source_target_pairs={{0,1},{1,0},{2,3},{3,2},{4,5},{5,4},{6,7},{7,6},{8,9},{9,8},{10,11... | collective-permute-start | bytes 135176 | tf_op jit(solution)/shard_map/ppermute | solution.py:323
  28.3 0.8 %copy-start.1 = (f32[88,128]{1,0:T(8,128)}, f32[88,128]{1,0:T(8,128)S(1)}, u32[]{:S(2)}) copy-start(f32[88,128]{1,0:T(8,128)S(1)} %collective-permute-done.1.peer) | copy-start | bytes 135172
  29.1 0.6 %copy-start.2 = (f32[88,128]{1,0:T(8,128)}, f32[88,128]{1,0:T(8,128)S(1)}, u32[]{:S(2)}) copy-start(f32[88,128]{1,0:T(8,128)S(1)} %collective-permute-done.mate) | copy-start | bytes 135172

commit v3 on v2

--- a/solution.py
+++ b/solution.py
@@ -5,6 +5,7 @@
 from jax.experimental import pallas as pl
 from jax.experimental.pallas import tpu as pltpu
 from jax.sharding import PartitionSpec as P
+
 
 LOG2E = 1.4426950408889634
 HI = lax.Precision.HIGHEST
@@ -41,6 +42,7 @@
         return 0
 
     lax.fori_loop(0, 30, spread, 0, unroll=2)
+
     def bcast(e, c):
         return tab[e, pl.ds(c, 8, stride=0), :][None]
 
@@ -150,7 +152,7 @@
         right[2 + i] = jnp.where(lane < 64, 0.0, t).astype(bf16)
         return 0
 
-    lax.fori_loop(0, 44, columns, 0, unroll=4)
+    lax.fori_loop(0, 44, columns, 0, unroll=11)
 
     def rows(e):
         hi, mid, lo = split3(ti[e])
@@ -196,8 +198,8 @@
         weights(8 + t, i, j, False)
         return 0
 
-    lax.fori_loop(0, 8, own_pair, 0)
-    lax.fori_loop(0, 7, rim_pair, 0)
+    lax.fori_loop(0, 8, own_pair, 0, unroll=8)
+    lax.fori_loop(0, 7, rim_pair, 0, unroll=7)
 
     total = sum(dsum[:, n, :] for n in range(8))
     h = com[CH, 9:39, :]
@@ -220,7 +222,7 @@
         out[i] = o[0:8] + o[8:16] + o[16:24]
         return 0
 
-    lax.fori_loop(0, 16, force, 0, unroll=2)
+    lax.fori_loop(0, 16, force, 0, unroll=8)
     s = com[CS, 16:32, :]
     scale = jnp.where(live[7:23], s * (-2.0 / LOG2E), 0.0)
     r = recip[7:23]
@@ -298,7 +300,7 @@
             pltpu.SMEM((3, 8, 128), f32),
             pltpu.SemaphoreType.DMA((3,)),
         ],
-        compiler_params=pltpu.CompilerParams(vmem_limit_bytes=56 << 20),
+        compiler_params=pltpu.CompilerParams(vmem_limit_bytes=40 << 20),
         name="sph",
     )(own, mate, peer)
 
@@ -319,8 +321,8 @@
     axes = ("curve", "group")
     chip = [(i, i ^ 1) for i in range(devices)]
     link = [(i, (i + 1 if i % 2 else i - 1) % devices) for i in range(devices)]
+    over_chip = lax.ppermute(packed, axes, chip)
     over_link = lax.ppermute(packed, axes, link)
-    over_chip = lax.ppermute(packed, axes, chip)
     return call(packed, over_chip, over_link, lambda: lax.rem(lax.axis_index("group"), 2))
 
 

time: 41.8 us -> 36.9 us (0.88)
  Pallas kernels: 11.7 us -> 7.53 us
  local copies, waits for them, and re-layouts: 1.97 us -> 1.35 us
    pallas_call x1, Pallas kernels: 11.7 us -> 7.53 us  [call(): pl.pallas_call(functools.partial(body, odd_of), out_shape=(jax.ShapeDtype...]
    unnamed x16 -> x10, local copies, waits for them, and re-layouts: 1.9 us -> 1.27 us
where the time goes in v3:
time: 36.9 us; the launch traced here: 36.7 us
  starting transfers between devices  26.2 us (71%)
  Pallas kernels  7.53 us (20%)
  local copies, waits for them, and re-layouts  1.35 us (4%)
  waiting for transfers between devices  0.85 us (2%)
  between operations  0.71 us (2%)
    ppermute x1, starting transfers between devices, shards(): over_chip = lax.ppermute(packed, axes, chip)  21.7 us
    pallas_call x1, Pallas kernels, call(): pl.pallas_call(functools.partial(body, odd_of), out_shape=(jax.ShapeDtype...  7.53 us
    ppermute x1, starting transfers between devices, shards(): over_link = lax.ppermute(packed, axes, link)  4.49 us
    unnamed x10, local copies, waits for them, and re-layouts  1.27 us
    ppermute x1, waiting for transfers between devices, shards(): over_chip = lax.ppermute(packed, axes, chip)  0.84 us
  transfers between devices with their start and end apart: 2, of which 1 were waited for; matrix products, arithmetic and copies ran while one was open for 0% of the time, Pallas kernels for 0%

profile of v3, /device:TPU:1, one launch (start us, length us, event | category | flops | bytes accessed | tf_op | source)
XLA Modules:
  0.0 36.7 jit_solution(4945038568367971946)
XLA Ops:
  0.6 0.0 copy-start.3
  0.6 0.0 copy-start.1
  0.7 0.0 copy-start.4
  0.7 0.0 copy-start
  0.7 0.6 %copy-done.3 = s32[128,8]{0,1:T(8,128)S(1)} copy-done((s32[128,8]{0,1:T(8,128)S(1)}, s32[128,8]{0,1:T(8,128)}, u32[]{:S(2)}) %copy-start.3) | copy-done | bytes 4120
  1.3 0.1 constant_dynamic-slice_fusion
  1.4 0.0 copy-done.1
  1.4 0.0 copy-done.4
  1.4 0.0 copy-start.2
  1.4 0.1 fusion
  1.5 0.0 copy-done
  1.5 0.6 %copy-done.2 = f32[16,128]{1,0:T(8,128)S(1)} copy-done((f32[16,128]{1,0:T(8,128)S(1)}, f32[16,128]{1,0:T(8,128)}, u32[]{:S(2)}) %copy-start.2) | copy-done | bytes 8216
  2.1 4.5 %collective-permute-start.1 = (f32[88,128]{1,0:T(8,128)S(1)}, f32[88,128]{1,0:T(8,128)S(1)}, u32[]{:S(2)}, u32[]{:S(2)}) collective-permute-start(f32[88,128]{1,0:T(8,128)S(1)} %select_maximum_fusion.own), channel_id=1, source_target_pairs={{0,1023},{1,2},{2,1},{3,4},{4,3},{5,6},{6,5},{7,8},{8,7},{9,10},{1... | collective-permute-start | bytes 135176 | tf_op jit(solution)/shard_map/ppermute | solution.py:325
  6.6 21.7 %collective-permute-start = (f32[88,128]{1,0:T(8,128)S(1)}, f32[88,128]{1,0:T(8,128)S(1)}, u32[]{:S(2)}, u32[]{:S(2)}) collective-permute-start(f32[88,128]{1,0:T(8,128)S(1)} %select_maximum_fusion.own), channel_id=1, source_target_pairs={{0,1},{1,0},{2,3},{3,2},{4,5},{5,4},{6,7},{7,6},{8,9},{9,8},{10,11... | collective-permute-start | bytes 135176 | tf_op jit(solution)/shard_map/ppermute | solution.py:324
  28.3 0.0 collective-permute-done.1.peer
  28.3 0.8 %collective-permute-done.mate = f32[88,128]{1,0:T(8,128)S(1)} collective-permute-done((f32[88,128]{1,0:T(8,128)S(1)}, f32[88,128]{1,0:T(8,128)S(1)}, u32[]{:S(2)}, u32[]{:S(2)}) %collective-permute-start) | collective-permute-done | bytes 45088 | tf_op jit(solution)/shard_map/ppermute | solution.py:324
  29.1 7.5 %sph.1 = (f32[16,128]{1,0:T(8,128)}, f32[3,16,128]{2,1,0:T(8,128)}) custom-call(f32[88,128]{1,0:T(8,128)S(1)} %select_maximum_fusion.own, f32[88,128]{1,0:T(8,128)S(1)} %collective-permute-done.mate, f32[88,128]{1,0:T(8,128)S(1)} %collective-permute-done.1.peer), custom_call_target="tpu_custom_call" | custom-call | tf_op jit(solution)/shard_map/sph/pallas_call | solution.py:278
  (3 shorter events, 0.0 us)
Async XLA Ops:
  0.6 0.7 %copy-start.3 = (s32[128,8]{0,1:T(8,128)S(1)}, s32[128,8]{0,1:T(8,128)}, u32[]{:S(2)}) copy-start(s32[128,8]{0,1:T(8,128)} %param.9) | copy-start | bytes 12292
  0.6 0.8 %copy-start.1 = (f32[16,128]{1,0:T(8,128)S(1)}, f32[16,128]{1,0:T(8,128)}, u32[]{:S(2)}) copy-start(f32[16,128]{1,0:T(8,128)} %param.6) | copy-start | bytes 24580
  0.7 0.8 %copy-start.4 = (s32[16]{0:T(128)S(1)}, s32[16]{0:T(128)}, u32[]{:S(2)}) copy-start(s32[16]{0:T(128)} %param.8) | copy-start | bytes 196
  0.7 0.8 %copy-start = (f32[3,16,128]{2,1,0:T(8,128)S(1)}, f32[3,16,128]{2,1,0:T(8,128)}, u32[]{:S(2)}) copy-start(f32[3,16,128]{2,1,0:T(8,128)} %param.5) | copy-start | bytes 73732
  1.4 0.7 %copy-start.2 = (f32[16,128]{1,0:T(8,128)S(1)}, f32[16,128]{1,0:T(8,128)}, u32[]{:S(2)}) copy-start(f32[16,128]{1,0:T(8,128)} %param.7) | copy-start | bytes 24580
  2.1 26.2 %collective-permute-start.1 = (f32[88,128]{1,0:T(8,128)S(1)}, f32[88,128]{1,0:T(8,128)S(1)}, u32[]{:S(2)}, u32[]{:S(2)}) collective-permute-start(f32[88,128]{1,0:T(8,128)S(1)} %select_maximum_fusion.own), channel_id=1, source_target_pairs={{0,1023},{1,2},{2,1},{3,4},{4,3},{5,6},{6,5},{7,8},{8,7},{9,10},{1... | collective-permute-start | bytes 135176 | tf_op jit(solution)/shard_map/ppermute | solution.py:325
  6.6 22.5 %collective-permute-start = (f32[88,128]{1,0:T(8,128)S(1)}, f32[88,128]{1,0:T(8,128)S(1)}, u32[]{:S(2)}, u32[]{:S(2)}) collective-permute-start(f32[88,128]{1,0:T(8,128)S(1)} %select_maximum_fusion.own), channel_id=1, source_target_pairs={{0,1},{1,0},{2,3},{3,2},{4,5},{5,4},{6,7},{7,6},{8,9},{9,8},{10,11... | collective-permute-start | bytes 135176 | tf_op jit(solution)/shard_map/ppermute | solution.py:324

commit v4 on v3

--- a/solution.py
+++ b/solution.py
@@ -152,7 +152,7 @@
         right[2 + i] = jnp.where(lane < 64, 0.0, t).astype(bf16)
         return 0
 
-    lax.fori_loop(0, 44, columns, 0, unroll=11)
+    lax.fori_loop(0, 44, columns, 0, unroll=22)
 
     def rows(e):
         hi, mid, lo = split3(ti[e])
@@ -222,7 +222,7 @@
         out[i] = o[0:8] + o[8:16] + o[16:24]
         return 0
 
-    lax.fori_loop(0, 16, force, 0, unroll=8)
+    lax.fori_loop(0, 16, force, 0, unroll=16)
     s = com[CS, 16:32, :]
     scale = jnp.where(live[7:23], s * (-2.0 / LOG2E), 0.0)
     r = recip[7:23]
@@ -319,10 +319,12 @@
     step = jnp.pad(step, ((0, 0), (0, slots - OWN)))
     packed = jnp.concatenate([position.reshape(3 * OWN, slots), mlive, smooth, step], 0)
     axes = ("curve", "group")
-    chip = [(i, i ^ 1) for i in range(devices)]
+    edge = [(0, 1), (1, 0)]
+    chip = [(i, i ^ 1) for i in range(2, devices)]
     link = [(i, (i + 1 if i % 2 else i - 1) % devices) for i in range(devices)]
-    over_chip = lax.ppermute(packed, axes, chip)
+    first = lax.ppermute(packed, axes, edge)
     over_link = lax.ppermute(packed, axes, link)
+    over_chip = first + lax.ppermute(packed, axes, chip)
     return call(packed, over_chip, over_link, lambda: lax.rem(lax.axis_index("group"), 2))
 
 

time: 36.9 us -> 35.1 us (0.951)
  the two profiles are of different devices: /device:TPU:1 before, /device:TPU:40 now
where the time goes in v4:
time: 35.1 us; the launch traced here: 34.8 us
  starting transfers between devices  23.9 us (68%)
  Pallas kernels  7.08 us (20%)
  waiting for transfers between devices  1.68 us (5%)
  local copies, waits for them, and re-layouts  1.35 us (4%)
  between operations  0.73 us (2%)
    ppermute x1, starting transfers between devices, shards(): over_link = lax.ppermute(packed, axes, link)  21.3 us
    pallas_call x1, Pallas kernels, call(): pl.pallas_call(functools.partial(body, odd_of), out_shape=(jax.ShapeDtype...  7.08 us
    ppermute x1, starting transfers between devices, shards(): over_chip = first + lax.ppermute(packed, axes, chip)  1.92 us
    ppermute x1, waiting for transfers between devices, shards(): over_link = lax.ppermute(packed, axes, link)  1.68 us
    unnamed x10, local copies, waits for them, and re-layouts  1.27 us
  transfers between devices with their start and end apart: 3, of which 1 were waited for; matrix products, arithmetic and copies ran while one was open for 0% of the time, Pallas kernels for 0%

profile of v4, /device:TPU:40, one launch (start us, length us, event | category | flops | bytes accessed | tf_op | source)
XLA Modules:
  0.0 34.8 jit_solution(1719088904720216558)
XLA Ops:
  0.6 0.0 copy-start.3
  0.6 0.0 copy-start.1
  0.7 0.0 copy-start.4
  0.7 0.0 copy-start
  0.7 0.6 %copy-done.3 = s32[128,8]{0,1:T(8,128)S(1)} copy-done((s32[128,8]{0,1:T(8,128)S(1)}, s32[128,8]{0,1:T(8,128)}, u32[]{:S(2)}) %copy-start.3) | copy-done | bytes 4120
  1.3 0.1 constant_dynamic-slice_fusion
  1.4 0.0 copy-done.1
  1.4 0.0 copy-done.4
  1.4 0.0 copy-start.2
  1.4 0.1 fusion
  1.5 0.0 copy-done
  1.5 0.6 %copy-done.2 = f32[16,128]{1,0:T(8,128)S(1)} copy-done((f32[16,128]{1,0:T(8,128)S(1)}, f32[16,128]{1,0:T(8,128)}, u32[]{:S(2)}) %copy-start.2) | copy-done | bytes 8216
  2.1 0.7 %collective-permute-start = (f32[88,128]{1,0:T(8,128)S(1)}, f32[88,128]{1,0:T(8,128)S(1)}, u32[]{:S(2)}, u32[]{:S(2)}) collective-permute-start(f32[88,128]{1,0:T(8,128)S(1)} %select_maximum_fusion.own), channel_id=1, source_target_pairs={{0,1},{1,0}} | collective-permute-start | bytes 135176 | tf_op jit(solution)/shard_map/ppermute | solution.py:325
  2.8 1.9 %collective-permute-start.1 = (f32[88,128]{1,0:T(8,128)S(1)}, f32[88,128]{1,0:T(8,128)S(1)}, u32[]{:S(2)}, u32[]{:S(2)}) collective-permute-start(f32[88,128]{1,0:T(8,128)S(1)} %select_maximum_fusion.own), channel_id=1, source_target_pairs={{2,3},{3,2},{4,5},{5,4},{6,7},{7,6},{8,9},{9,8},{10,11},{11,10},{1... | collective-permute-start | bytes 135176 | tf_op jit(solution)/shard_map/ppermute | solution.py:327
  4.7 21.3 %collective-permute-start.2 = (f32[88,128]{1,0:T(8,128)S(1)}, f32[88,128]{1,0:T(8,128)S(1)}, u32[]{:S(2)}, u32[]{:S(2)}) collective-permute-start(f32[88,128]{1,0:T(8,128)S(1)} %select_maximum_fusion.own), channel_id=1, source_target_pairs={{0,1023},{1,2},{2,1},{3,4},{4,3},{5,6},{6,5},{7,8},{8,7},{9,10},{1... | collective-permute-start | bytes 135176 | tf_op jit(solution)/shard_map/ppermute | solution.py:326
  26.0 0.0 collective-permute-done
  26.0 0.0 collective-permute-done.1
  26.1 1.7 %collective-permute-done.2.peer = f32[88,128]{1,0:T(8,128)S(1)} collective-permute-done((f32[88,128]{1,0:T(8,128)S(1)}, f32[88,128]{1,0:T(8,128)S(1)}, u32[]{:S(2)}, u32[]{:S(2)}) %collective-permute-start.2) | collective-permute-done | bytes 45088 | tf_op jit(solution)/shard_map/ppermute | solution.py:326
  27.7 7.1 %sph.1 = (f32[16,128]{1,0:T(8,128)}, f32[3,16,128]{2,1,0:T(8,128)}) custom-call(f32[88,128]{1,0:T(8,128)S(1)} %select_maximum_fusion.own, f32[88,128]{1,0:T(8,128)S(1)} %add.26.mate, f32[88,128]{1,0:T(8,128)S(1)} %collective-permute-done.2.peer), custom_call_target="tpu_custom_call" | custom-call | tf_op jit(solution)/shard_map/sph/pallas_call | solution.py:278
  (4 shorter events, 0.0 us)
Async XLA Ops:
  0.6 0.7 %copy-start.3 = (s32[128,8]{0,1:T(8,128)S(1)}, s32[128,8]{0,1:T(8,128)}, u32[]{:S(2)}) copy-start(s32[128,8]{0,1:T(8,128)} %param.9) | copy-start | bytes 12292
  0.6 0.8 %copy-start.1 = (f32[16,128]{1,0:T(8,128)S(1)}, f32[16,128]{1,0:T(8,128)}, u32[]{:S(2)}) copy-start(f32[16,128]{1,0:T(8,128)} %param.6) | copy-start | bytes 24580
  0.7 0.8 %copy-start.4 = (s32[16]{0:T(128)S(1)}, s32[16]{0:T(128)}, u32[]{:S(2)}) copy-start(s32[16]{0:T(128)} %param.8) | copy-start | bytes 196
  0.7 0.8 %copy-start = (f32[3,16,128]{2,1,0:T(8,128)S(1)}, f32[3,16,128]{2,1,0:T(8,128)}, u32[]{:S(2)}) copy-start(f32[3,16,128]{2,1,0:T(8,128)} %param.5) | copy-start | bytes 73732
  1.4 0.7 %copy-start.2 = (f32[16,128]{1,0:T(8,128)S(1)}, f32[16,128]{1,0:T(8,128)}, u32[]{:S(2)}) copy-start(f32[16,128]{1,0:T(8,128)} %param.7) | copy-start | bytes 24580
  2.1 23.9 %collective-permute-start = (f32[88,128]{1,0:T(8,128)S(1)}, f32[88,128]{1,0:T(8,128)S(1)}, u32[]{:S(2)}, u32[]{:S(2)}) collective-permute-start(f32[88,128]{1,0:T(8,128)S(1)} %select_maximum_fusion.own), channel_id=1, source_target_pairs={{0,1},{1,0}} | collective-permute-start | bytes 135176 | tf_op jit(solution)/shard_map/ppermute | solution.py:325
  2.8 23.3 %collective-permute-start.1 = (f32[88,128]{1,0:T(8,128)S(1)}, f32[88,128]{1,0:T(8,128)S(1)}, u32[]{:S(2)}, u32[]{:S(2)}) collective-permute-start(f32[88,128]{1,0:T(8,128)S(1)} %select_maximum_fusion.own), channel_id=1, source_target_pairs={{2,3},{3,2},{4,5},{5,4},{6,7},{7,6},{8,9},{9,8},{10,11},{11,10},{1... | collective-permute-start | bytes 135176 | tf_op jit(solution)/shard_map/ppermute | solution.py:327
  4.7 23.0 %collective-permute-start.2 = (f32[88,128]{1,0:T(8,128)S(1)}, f32[88,128]{1,0:T(8,128)S(1)}, u32[]{:S(2)}, u32[]{:S(2)}) collective-permute-start(f32[88,128]{1,0:T(8,128)S(1)} %select_maximum_fusion.own), channel_id=1, source_target_pairs={{0,1023},{1,2},{2,1},{3,4},{4,3},{5,6},{6,5},{7,8},{8,7},{9,10},{1... | collective-permute-start | bytes 135176 | tf_op jit(solution)/shard_map/ppermute | solution.py:326

commit v5 on v4

--- a/solution.py
+++ b/solution.py
@@ -319,8 +319,9 @@
     step = jnp.pad(step, ((0, 0), (0, slots - OWN)))
     packed = jnp.concatenate([position.reshape(3 * OWN, slots), mlive, smooth, step], 0)
     axes = ("curve", "group")
-    edge = [(0, 1), (1, 0)]
-    chip = [(i, i ^ 1) for i in range(2, devices)]
+    lap = 16 * groups
+    edge = [(i, i ^ 1) for i in range(devices) if i % lap < 2]
+    chip = [(i, i ^ 1) for i in range(devices) if i % lap >= 2]
     link = [(i, (i + 1 if i % 2 else i - 1) % devices) for i in range(devices)]
     first = lax.ppermute(packed, axes, edge)
     over_link = lax.ppermute(packed, axes, link)

time: 35.1 us -> 35.1 us (level)
    ppermute x1, starting transfers between devices: 1.92 us -> 0.66 us  [shards(): over_chip = first + lax.ppermute(packed, axes, chip)]
    ppermute x1, starting transfers between devices: 0.65 us -> 1.91 us  [shards(): first = lax.ppermute(packed, axes, edge)]
where the time goes in v5:
time: 35.1 us; the launch traced here: 34.8 us
  starting transfers between devices  23.9 us (68%)
  Pallas kernels  7.08 us (20%)
  waiting for transfers between devices  1.68 us (5%)
  local copies, waits for them, and re-layouts  1.35 us (4%)
  between operations  0.73 us (2%)
    ppermute x1, starting transfers between devices, shards(): over_link = lax.ppermute(packed, axes, link)  21.3 us
    pallas_call x1, Pallas kernels, call(): pl.pallas_call(functools.partial(body, odd_of), out_shape=(jax.ShapeDtype...  7.08 us
    ppermute x1, starting transfers between devices, shards(): first = lax.ppermute(packed, axes, edge)  1.91 us
    ppermute x1, waiting for transfers between devices, shards(): over_link = lax.ppermute(packed, axes, link)  1.68 us
    unnamed x10, local copies, waits for them, and re-layouts  1.27 us
  transfers between devices with their start and end apart: 3, of which 1 were waited for; matrix products, arithmetic and copies ran while one was open for 0% of the time, Pallas kernels for 0%

profile of v5, /device:TPU:40, one launch (start us, length us, event | category | flops | bytes accessed | tf_op | source)
XLA Modules:
  0.0 34.8 jit_solution(3917408497208648271)
XLA Ops:
  0.6 0.0 copy-start.3
  0.6 0.0 copy-start.1
  0.7 0.0 copy-start.4
  0.7 0.0 copy-start
  0.7 0.6 %copy-done.3 = s32[128,8]{0,1:T(8,128)S(1)} copy-done((s32[128,8]{0,1:T(8,128)S(1)}, s32[128,8]{0,1:T(8,128)}, u32[]{:S(2)}) %copy-start.3) | copy-done | bytes 4120
  1.3 0.1 constant_dynamic-slice_fusion
  1.4 0.0 copy-done.1
  1.4 0.0 copy-done.4
  1.4 0.0 copy-start.2
  1.4 0.1 fusion
  1.5 0.0 copy-done
  1.5 0.6 %copy-done.2 = f32[16,128]{1,0:T(8,128)S(1)} copy-done((f32[16,128]{1,0:T(8,128)S(1)}, f32[16,128]{1,0:T(8,128)}, u32[]{:S(2)}) %copy-start.2) | copy-done | bytes 8216
  2.1 1.9 %collective-permute-start = (f32[88,128]{1,0:T(8,128)S(1)}, f32[88,128]{1,0:T(8,128)S(1)}, u32[]{:S(2)}, u32[]{:S(2)}) collective-permute-start(f32[88,128]{1,0:T(8,128)S(1)} %select_maximum_fusion.own), channel_id=1, source_target_pairs={{0,1},{1,0},{128,129},{129,128},{256,257},{257,256},{384,385},{385... | collective-permute-start | bytes 135176 | tf_op jit(solution)/shard_map/ppermute | solution.py:326
  4.0 0.7 %collective-permute-start.1 = (f32[88,128]{1,0:T(8,128)S(1)}, f32[88,128]{1,0:T(8,128)S(1)}, u32[]{:S(2)}, u32[]{:S(2)}) collective-permute-start(f32[88,128]{1,0:T(8,128)S(1)} %select_maximum_fusion.own), channel_id=1, source_target_pairs={{2,3},{3,2},{4,5},{5,4},{6,7},{7,6},{8,9},{9,8},{10,11},{11,10},{1... | collective-permute-start | bytes 135176 | tf_op jit(solution)/shard_map/ppermute | solution.py:328
  4.7 21.3 %collective-permute-start.2 = (f32[88,128]{1,0:T(8,128)S(1)}, f32[88,128]{1,0:T(8,128)S(1)}, u32[]{:S(2)}, u32[]{:S(2)}) collective-permute-start(f32[88,128]{1,0:T(8,128)S(1)} %select_maximum_fusion.own), channel_id=1, source_target_pairs={{0,1023},{1,2},{2,1},{3,4},{4,3},{5,6},{6,5},{7,8},{8,7},{9,10},{1... | collective-permute-start | bytes 135176 | tf_op jit(solution)/shard_map/ppermute | solution.py:327
  26.0 0.0 collective-permute-done
  26.0 0.0 collective-permute-done.1
  26.1 1.7 %collective-permute-done.2.peer = f32[88,128]{1,0:T(8,128)S(1)} collective-permute-done((f32[88,128]{1,0:T(8,128)S(1)}, f32[88,128]{1,0:T(8,128)S(1)}, u32[]{:S(2)}, u32[]{:S(2)}) %collective-permute-start.2) | collective-permute-done | bytes 45088 | tf_op jit(solution)/shard_map/ppermute | solution.py:327
  27.7 7.1 %sph.1 = (f32[16,128]{1,0:T(8,128)}, f32[3,16,128]{2,1,0:T(8,128)}) custom-call(f32[88,128]{1,0:T(8,128)S(1)} %select_maximum_fusion.own, f32[88,128]{1,0:T(8,128)S(1)} %add.26.mate, f32[88,128]{1,0:T(8,128)S(1)} %collective-permute-done.2.peer), custom_call_target="tpu_custom_call" | custom-call | tf_op jit(solution)/shard_map/sph/pallas_call | solution.py:278
  (4 shorter events, 0.0 us)
Async XLA Ops:
  0.6 0.7 %copy-start.3 = (s32[128,8]{0,1:T(8,128)S(1)}, s32[128,8]{0,1:T(8,128)}, u32[]{:S(2)}) copy-start(s32[128,8]{0,1:T(8,128)} %param.9) | copy-start | bytes 12292
  0.6 0.8 %copy-start.1 = (f32[16,128]{1,0:T(8,128)S(1)}, f32[16,128]{1,0:T(8,128)}, u32[]{:S(2)}) copy-start(f32[16,128]{1,0:T(8,128)} %param.6) | copy-start | bytes 24580
  0.7 0.8 %copy-start.4 = (s32[16]{0:T(128)S(1)}, s32[16]{0:T(128)}, u32[]{:S(2)}) copy-start(s32[16]{0:T(128)} %param.8) | copy-start | bytes 196
  0.7 0.8 %copy-start = (f32[3,16,128]{2,1,0:T(8,128)S(1)}, f32[3,16,128]{2,1,0:T(8,128)}, u32[]{:S(2)}) copy-start(f32[3,16,128]{2,1,0:T(8,128)} %param.5) | copy-start | bytes 73732
  1.4 0.7 %copy-start.2 = (f32[16,128]{1,0:T(8,128)S(1)}, f32[16,128]{1,0:T(8,128)}, u32[]{:S(2)}) copy-start(f32[16,128]{1,0:T(8,128)} %param.7) | copy-start | bytes 24580
  2.1 23.9 %collective-permute-start = (f32[88,128]{1,0:T(8,128)S(1)}, f32[88,128]{1,0:T(8,128)S(1)}, u32[]{:S(2)}, u32[]{:S(2)}) collective-permute-start(f32[88,128]{1,0:T(8,128)S(1)} %select_maximum_fusion.own), channel_id=1, source_target_pairs={{0,1},{1,0},{128,129},{129,128},{256,257},{257,256},{384,385},{385... | collective-permute-start | bytes 135176 | tf_op jit(solution)/shard_map/ppermute | solution.py:326
  4.0 22.0 %collective-permute-start.1 = (f32[88,128]{1,0:T(8,128)S(1)}, f32[88,128]{1,0:T(8,128)S(1)}, u32[]{:S(2)}, u32[]{:S(2)}) collective-permute-start(f32[88,128]{1,0:T(8,128)S(1)} %select_maximum_fusion.own), channel_id=1, source_target_pairs={{2,3},{3,2},{4,5},{5,4},{6,7},{7,6},{8,9},{9,8},{10,11},{11,10},{1... | collective-permute-start | bytes 135176 | tf_op jit(solution)/shard_map/ppermute | solution.py:328
  4.7 23.0 %collective-permute-start.2 = (f32[88,128]{1,0:T(8,128)S(1)}, f32[88,128]{1,0:T(8,128)S(1)}, u32[]{:S(2)}, u32[]{:S(2)}) collective-permute-start(f32[88,128]{1,0:T(8,128)S(1)} %select_maximum_fusion.own), channel_id=1, source_target_pairs={{0,1023},{1,2},{2,1},{3,4},{4,3},{5,6},{6,5},{7,8},{8,7},{9,10},{1... | collective-permute-start | bytes 135176 | tf_op jit(solution)/shard_map/ppermute | solution.py:327
